TPU v7x, 512 devices: a whole 4x4x16 slice. The times are simulated.
512 devices in a mesh: row: 16 (over x, y), col: 32 (over z, core).
Axes of the slice: x: 4, y: 4, z: 16, core: 2. Of those that a mesh axis runs over, the one named last changes fastest.
Arguments:
- start_vector: bfloat16 [4, 2048, 2048], P(None, 'row', 'col'), may hold values from -150 to 150
- left_env: bfloat16 [5, 2048, 2048], P(None, 'row', 'col'), may hold values from -5 to 6
- right_env: bfloat16 [5, 2048, 2048], P(None, 'col', 'row'), may hold values from -5 to 6
- left_tensor: float32 [5, 5, 2, 2], replicated, may hold values from -1.5 to 2.5
- right_tensor: float32 [5, 5, 2, 2], replicated, may hold values from -1.5 to 2.5
Outputs:
- next_vector: bfloat16 [4, 2048, 2048], P(None, 'row', 'col')
- coefficients: float32 [2], replicated
All inputs are finite; a program needn't handle non-finite values.
Results may differ from a plain program's by a relative error of at most 0.023.
Values may be sent and summed in bfloat16 or wider, within the bound.
No kernel may reach another device: no remote copies, remote signals or barrier semaphores. Data moves between devices by JAX's collectives and lax.ppermute only.
A program may use at most 64 MiB of HBM per device.

v0:
```python
import jax
import jax.numpy as jnp
from jax import lax
from jax.sharding import Mesh
from jax.sharding import PartitionSpec as P

ROW = ("row_0", "row_1")
COL = ("col_0", "col_1")
ROW_COL = ("row_0", "row_1", "col_0", "col_1")
epsilon = 1e-06


def copy_for_each(x, axis):
    size = lax.axis_size(axis)
    return lax.all_to_all(jnp.broadcast_to(x[None], (size, *x.shape)), axis, 0, 0, tiled=True)


def joined_along(pieces, dim):
    pieces = jnp.moveaxis(pieces, 0, dim)
    lengths = pieces.shape
    return pieces.reshape(*lengths[:dim], lengths[dim] * lengths[dim + 1], *lengths[dim + 2 :])


def gathered_copies(x, axis, dim):
    pieces = copy_for_each(x, axis)
    return joined_along(pieces, dim)


def sum_in_order(pieces, axes, sequence):
    lengths = [lax.axis_size(a) for a in axes]
    pieces = pieces.reshape(*lengths, *pieces.shape[1:])
    pieces = pieces.transpose(*sequence, *range(len(axes), pieces.ndim))
    pieces = pieces.reshape(-1, *pieces.shape[len(axes) :])
    for k in sequence:
        pieces = lax.psum_scatter(pieces, axes[k], scatter_dimension=0, tiled=True)
    return pieces[0]


def cut_along(x, dim, size):
    lengths = x.shape
    pieces = x.reshape(*lengths[:dim], size, lengths[dim] // size, *lengths[dim + 1 :])
    return jnp.moveaxis(pieces, dim, 0)


def scatter_axes(x, axes, sequence, dim):
    size = lax.axis_size(axes)
    return sum_in_order(cut_along(x, dim, size), axes, sequence)


def by_axis(x, axes):
    for axis in axes:
        x = lax.psum(x, axis)
    return x


def coupling(left_tensor, right_tensor):
    channels = left_tensor.shape[0]
    joined = jnp.einsum(
        "wuac,uvbd->vabwcd", left_tensor, right_tensor, precision=lax.Precision.HIGHEST
    )
    return joined.reshape(channels, 4, channels, 4)


def contract_left(portion, columns):
    return jnp.einsum("wax,txb->wtba", portion, columns, preferred_element_type=jnp.float32)


def mix_channels(coupling_table, cross):
    mixed_bond = jnp.einsum(
        "vswt,wtba->vsba", coupling_table, cross, precision=lax.Precision.HIGHEST
    )
    return mixed_bond.astype(jnp.bfloat16)


def contract_right(mixed_bond, portion):
    return jnp.einsum("vsba,vbc->sac", mixed_bond, portion, preferred_element_type=jnp.float32)


def apply_hamiltonian(vector, coupling_table, panels):
    columns = gathered_copies(vector, ROW, 1)
    cross = contract_left(panels[0], columns)
    mixed_bond = mix_channels(coupling_table, cross)
    partials = contract_right(mixed_bond, panels[1])
    return scatter_axes(partials.astype(jnp.bfloat16), COL, (1, 0), 2).astype(jnp.float32)


def local_mean(former, latter, entries):
    return jnp.sum(former * latter) / entries


def body(start_vector, left_env, right_env, left_tensor, right_tensor):
    coupling_table = coupling(left_tensor, right_tensor)
    entries = float(
        start_vector.shape[0]
        * start_vector.shape[1]
        * start_vector.shape[2]
        * lax.axis_size(ROW)
        * lax.axis_size(COL)
    )
    panels = (lax.all_gather(left_env, COL, axis=2, tiled=True), gathered_copies(right_env, ROW, 2))
    base_vector = start_vector.astype(jnp.float32)
    image = apply_hamiltonian(start_vector, coupling_table, panels)
    base_square, correlation, image_square = (
        by_axis(local_mean(base_vector, base_vector, entries), ROW_COL),
        by_axis(local_mean(base_vector, image, entries), ROW_COL),
        by_axis(local_mean(image, image, entries), ROW_COL),
    )
    alpha = correlation / (base_square + epsilon)
    residual = image - alpha * base_vector
    rho = jnp.sqrt(image_square - 2.0 * alpha * correlation + alpha * alpha * base_square + epsilon)
    next_vector = (residual / rho).astype(jnp.bfloat16)
    coefficients = jnp.stack([alpha, rho])
    return (next_vector, coefficients)


def solution(mesh):
    finer = Mesh(mesh.devices.reshape(4, 4, 16, 2), ("row_0", "row_1", "col_0", "col_1"))
    in_specs = (P(None, ROW, COL), P(None, ROW, COL), P(None, COL, ROW), P(), P())
    out_specs = (P(None, ROW, COL), P())
    return jax.shard_map(body, mesh=finer, in_specs=in_specs, out_specs=out_specs, check_vma=False)
```

profile of v0, /device:TPU:1, one launch (start us, length us, event | category | flops | bytes accessed | tf_op | source)
XLA Modules:
  0.0 263.9 jit_solution(11655160880378192590)
XLA Ops:
  7.2 0.7 all-gather.2.cloned.1.call-update
  7.9 1.1 broadcast_in_dim.4
  9.0 22.4 %all_to_all.10 = bf16[16,4,128,64]{2,3,1,0:T(8,128)(2,1)S(1)} all-to-all(bf16[16,4,128,64]{2,3,1,0:T(8,128)(2,1)S(1)} %broadcast_in_dim.4), channel_id=1, replica_groups=mesh['row_0'=4,'row_1'=4,'col_0'=16,'col_1'=2] {'row_0','row_1'}, dimensions={0} | all-to-all | bytes 2097152 | tf_op jit(solution)/shard_map/all_to_all | solution.py:15
  31.4 1.4 broadcast_in_dim.5
  32.8 3.7 %all-to-all-start.1 = ((bf16[16,5,64,128]{3,2,1,0:T(8,128)(2,1)}), bf16[16,5,64,128]{3,2,1,0:T(8,128)(2,1)S(1)}, u32[]{:S(2)}, u32[]{:S(2)}) async-start(bf16[16,5,64,128]{3,2,1,0:T(8,128)(2,1)} %broadcast_in_dim.5), calls=%async_computation.1 | async-start | bytes 2621440 | tf_op jit(solution)/shard_map/all_to_all | solution.py:15
  37.0 0.7 copy.19
  37.7 1.3 reshape.35
  39.0 14.3 %all-to-all-done.1 = bf16[16,5,64,128]{3,2,1,0:T(8,128)(2,1)S(1)} async-done(((bf16[16,5,64,128]{3,2,1,0:T(8,128)(2,1)}), bf16[16,5,64,128]{3,2,1,0:T(8,128)(2,1)S(1)}, u32[]{:S(2)}, u32[]{:S(2)}) %all-to-all-start.1) | async-done | bytes 1310752 | tf_op jit(solution)/shard_map/all_to_all | solution.py:15
  53.3 0.9 copy.22
  54.2 0.6 reshape.40
  54.8 33.2 %all-gather.2.cloned.1.call-done = bf16[5,128,2048]{1,2,0:T(8,128)(2,1)} async-done(((bf16[5,128,64]{1,2,0:T(8,128)(2,1)}), bf16[5,128,2048]{1,2,0:T(8,128)(2,1)}) %all-gather.2.cloned.1.call-update) | async-done | bytes 2621456 | tf_op jit(solution)/shard_map/all_gather | solution.py:100
  88.0 3.0 %fusion.3 = f32[5,4,64,128]{3,2,0,1:T(8,128)S(1)} fusion(bf16[5,128,2048]{1,2,0:T(8,128)(2,1)} %all-gather.2.cloned.1.call-done, bf16[4,2048,64,1]{1,2,0,3:T(8,128)(2,1)} %reshape.35), kind=kOutput, calls=%fused_computation.5 | convolution fusion | flops 671088640 | bytes 4325376 | tf_op jit(solution)/shard_map/wax,txb->wtba/dot_general | solution.py:65
  91.1 4.0 %fusion.2 = bf16[5,4,64,128]{3,0,2,1:T(8,128)(2,1)S(1)} fusion(f32[5,4,64,128]{3,2,0,1:T(8,128)S(1)} %fusion.3, f32[5,4,5,4,1]{2,3,1,0,4:T(4,128)S(1)} %bitcast.57), kind=kOutput, calls=%fused_computation.4 | convolution fusion | flops 39485440 | bytes 984640 | tf_op jit(solution)/shard_map/vswt,wtba->vsba/dot_general | solution.py:69
  95.1 1.3 bitcast_convert_fusion
  96.4 2.5 copy.24
  98.9 3.2 %copy.25 = bf16[2,16,4,128,64]{3,4,2,1,0:T(8,128)(2,1)} copy(bf16[2,16,4,128,64]{3,4,0,1,2:T(8,128)(2,1)} %bitcast.54) | data formatting | bytes 4194304 | tf_op jit(solution)/shard_map/transpose | solution.py:32
  102.1 17.6 %reduce-scatter.3.cloned.1.call-done = bf16[16,4,128,64]{2,3,1,0:T(8,128)(2,1)} async-done(((bf16[32,4,128,64]{2,3,1,0:T(8,128)(2,1)}), bf16[16,4,128,64]{2,3,1,0:T(8,128)(2,1)}) %reduce-scatter.3.cloned.1.call-update) | async-done | bytes 1048592 | tf_op jit(solution)/shard_map/reduce_scatter | solution.py:35
  119.8 64.3 %reduce-scatter.5.cloned.1.call-done = bf16[1,4,128,64]{2,3,1,0:T(8,128)(2,1)} async-done(((bf16[16,4,128,64]{2,3,1,0:T(8,128)(2,1)}), bf16[1,4,128,64]{2,3,1,0:T(8,128)(2,1)}) %reduce-scatter.5.cloned.1.call-update) | async-done | bytes 65552 | tf_op jit(solution)/shard_map/reduce_scatter | solution.py:35
  184.0 1.5 fusion.10
  187.5 9.5 %all-reduce.2 = (f32[]{:T(128)}, f32[]{:T(128)}, f32[]{:T(128)}) all-reduce(f32[]{:T(128)S(6)} %div.21, f32[]{:T(128)S(6)} %div.18, f32[]{:T(128)S(6)} %div.19), channel_id=1, replica_groups=mesh['row_0'=4,'row_1'=4,'col_0'=16,'col_1'=2] {'row_0'}, use_global_device_ids=true, to_apply=%region_13.0 | all-reduce | flops 3 | bytes 24 | tf_op jit(solution)/shard_map/psum | solution.py:52
  196.9 8.5 %all-reduce.1 = (f32[]{:T(128)}, f32[]{:T(128)}, f32[]{:T(128)}) all-reduce(f32[]{:T(128)} %get-tuple-element.11, f32[]{:T(128)} %get-tuple-element.12, f32[]{:T(128)} %get-tuple-element.13), channel_id=1, replica_groups=mesh['row_0'=4,'row_1'=4,'col_0'=16,'col_1'=2] {'row_1'}, use_global_device_ids=true, to_apply=%region_14.0 | all-reduce | flops 3 | bytes 24 | tf_op jit(solution)/shard_map/psum | solution.py:52
  205.5 22.2 %all-reduce = (f32[]{:T(128)}, f32[]{:T(128)}, f32[]{:T(128)}) all-reduce(f32[]{:T(128)} %get-tuple-element.8, f32[]{:T(128)} %get-tuple-element.9, f32[]{:T(128)} %get-tuple-element.10), channel_id=1, replica_groups=mesh['row_0'=4,'row_1'=4,'col_0'=16,'col_1'=2] {'col_0'}, use_global_device_ids=true, to_apply=%region_15.0 | all-reduce | flops 3 | bytes 24 | tf_op jit(solution)/shard_map/psum | solution.py:52
  227.7 24.4 %all-reduce.3 = (f32[]{:T(128)}, f32[]{:T(128)}, f32[]{:T(128)}) all-reduce(f32[]{:T(128)} %get-tuple-element.5, f32[]{:T(128)} %get-tuple-element.6, f32[]{:T(128)} %get-tuple-element.7), channel_id=1, replica_groups=mesh['row_0'=4,'row_1'=4,'col_0'=16,'col_1'=2] {'col_1'}, use_global_device_ids=true, to_apply=%region_16.0 | all-reduce | flops 3 | bytes 24 | tf_op jit(solution)/shard_map/psum | solution.py:52
  255.8 1.5 fusion.13
  (16 shorter events, 1.2 us)
Async XLA Ops:
  7.2 29.4 %copy-start = (f32[5,5,2,2]{1,3,2,0:T(2,128)S(1)}, f32[5,5,2,2]{1,3,2,0:T(2,128)}, u32[]{:S(2)}) copy-start(f32[5,5,2,2]{1,3,2,0:T(2,128)} %param.8) | copy-start | bytes 1204
  7.2 24.2 %copy-start.2 = (bf16[5,64,128]{2,1,0:T(8,128)(2,1)S(1)}, bf16[5,64,128]{2,1,0:T(8,128)(2,1)}, u32[]{:S(2)}) copy-start(bf16[5,64,128]{2,1,0:T(8,128)(2,1)} %param.7) | copy-start | bytes 245764
  7.2 80.8 %all-gather.2.cloned.1.call-start = ((), (), s32[]{:S(2)}) async-start(), calls=%async_computation.4 | async-start | bytes 2703360 | tf_op jit(solution)/shard_map/all_gather | solution.py:100
  31.4 5.2 %copy-start.3 = (f32[5,5,2,2]{1,3,2,0:T(2,128)S(1)}, f32[5,5,2,2]{1,3,2,0:T(2,128)}, u32[]{:S(2)}) copy-start(f32[5,5,2,2]{1,3,2,0:T(2,128)} %param.9) | copy-start | bytes 1204
  32.8 20.5 %all-to-all-start.1 = ((bf16[16,5,64,128]{3,2,1,0:T(8,128)(2,1)}), bf16[16,5,64,128]{3,2,1,0:T(8,128)(2,1)S(1)}, u32[]{:S(2)}, u32[]{:S(2)}) async-start(bf16[16,5,64,128]{3,2,1,0:T(8,128)(2,1)} %broadcast_in_dim.5), calls=%async_computation.1 | async-start | bytes 2621440 | tf_op jit(solution)/shard_map/all_to_all | solution.py:15
  36.5 83.2 %reduce-scatter.3.cloned.1.call-start = ((), (), s32[]{:S(2)}) async-start(), calls=%async_computation.5 | async-start | bytes 3145728 | tf_op jit(solution)/shard_map/reduce_scatter | solution.py:35
  102.1 82.0 %copy-start.1 = (bf16[4,128,64]{1,2,0:T(8,128)(2,1)S(1)}, bf16[4,128,64]{1,2,0:T(8,128)(2,1)}, u32[]{:S(2)}) copy-start(bf16[4,128,64]{1,2,0:T(8,128)(2,1)} %param.5) | copy-start | bytes 196612
  102.1 82.0 %reduce-scatter.5.cloned.1.call-start = ((), (), s32[]{:S(2)}) async-start(), calls=%async_computation.6 | async-start | bytes 1114112 | tf_op jit(solution)/shard_map/reduce_scatter | solution.py:35
Sparse Core Ops, SparseCore 0:
  10.1 77.8 all-gather.1
  102.2 17.5 reduce-scatter.2
  122.6 61.4 reduce-scatter.4
where the time goes:
time: 264 us
  waiting for transfers between devices  130 us (49%)
  blocking collectives  87.1 us (33%)
  between operations  18.9 us (7%)
  local copies, waits for them, and re-layouts  11.7 us (4%)
  matrix products  8.74 us (3%)
  starting transfers between devices  3.82 us (1%)
  other arithmetic  3.6 us (1%)
    reduce_scatter x2, waiting for transfers between devices, sum_in_order(): pieces = lax.psum_scatter(pieces, axes[k], scatter_dimension=0, tiled=True)  81.9 us
    psum x4, blocking collectives, by_axis(): x = lax.psum(x, axis)  64.7 us
    all_gather x1, waiting for transfers between devices, body(): lax.all_gather(left_env, COL, axis=2, tiled=True)  33.2 us
    all_to_all x1, blocking collectives, copy_for_each(): lax.all_to_all(jnp.broadcast_to(x[None], (size, *x.shape)), axis, 0, 0, t...  22.4 us
    all_to_all x1, waiting for transfers between devices, copy_for_each(): lax.all_to_all(jnp.broadcast_to(x[None], (size, *x.shape)), axis, 0, 0, t...  14.3 us
  transfers between devices with their start and end apart: 4, of which 4 were waited for; matrix products, arithmetic and copies ran while one was open for 2% of the time, Pallas kernels for 0%

commit v1 on v0

--- a/solution.py
+++ b/solution.py
@@ -49,7 +49,8 @@
 
 def by_axis(x, axes):
     for axis in axes:
-        x = lax.psum(x, axis)
+        parts = lax.all_gather(x, axis, axis=0, tiled=False)
+        x = parts.sum(axis=0)
     return x
 
 

time: 264 us -> 287 us (1.087)
  local copies, waits for them, and re-layouts: 11.7 us -> 31.3 us
  other arithmetic: 3.6 us -> 10.8 us
    psum x4 -> x0, blocking collectives: 64.7 us -> none  [by_axis(): x = lax.psum(x, axis)]
    unnamed x0 -> x4, blocking collectives: none -> 62.2 us
    unnamed x8 -> x36, local copies, waits for them, and re-layouts: 0.02 us -> 19.6 us
    reduce_sum x0 -> x12, other arithmetic: none -> 7.21 us  [by_axis(): x = parts.sum(axis=0)]
  transfers between devices with their start and end apart: 4 -> 4, of which waited for: 4 -> 4; matrix products, arithmetic and copies ran while one was open for 2% -> 3% of each run, Pallas kernels for 0% -> 0%
where the time goes in v1:
time: 287 us; the launch traced here: 286 us
  waiting for transfers between devices  128 us (45%)
  blocking collectives  84.6 us (29%)
  local copies, waits for them, and re-layouts  31.3 us (11%)
  between operations  19 us (7%)
  other arithmetic  10.8 us (4%)
  matrix products  8.74 us (3%)
  starting transfers between devices  3.82 us (1%)
    reduce_scatter x2, waiting for transfers between devices, sum_in_order(): pieces = lax.psum_scatter(pieces, axes[k], scatter_dimension=0, tiled=True)  79.3 us
    unnamed x4, blocking collectives  62.2 us
    all_gather x1, waiting for transfers between devices, body(): lax.all_gather(left_env, COL, axis=2, tiled=True)  33.2 us
    all_to_all x1, blocking collectives, copy_for_each(): lax.all_to_all(jnp.broadcast_to(x[None], (size, *x.shape)), axis, 0, 0, t...  22.4 us
    unnamed x36, local copies, waits for them, and re-layouts  19.6 us
    all_to_all x1, waiting for transfers between devices, copy_for_each(): lax.all_to_all(jnp.broadcast_to(x[None], (size, *x.shape)), axis, 0, 0, t...  14.3 us
    reduce_sum x12, other arithmetic, by_axis(): x = parts.sum(axis=0)  7.21 us
  transfers between devices with their start and end apart: 4, of which 4 were waited for; matrix products, arithmetic and copies ran while one was open for 3% of the time, Pallas kernels for 0%

profile of v1, /device:TPU:1, one launch (start us, length us, event | category | flops | bytes accessed | tf_op | source)
XLA Modules:
  0.0 285.8 jit_solution(2255250919447697174)
XLA Ops:
  9.0 22.4 %all_to_all.10 = bf16[16,4,128,64]{2,3,1,0:T(8,128)(2,1)S(1)} all-to-all(bf16[16,4,128,64]{2,3,1,0:T(8,128)(2,1)S(1)} %broadcast_in_dim.4), channel_id=1, replica_groups=mesh['row_0'=4,'row_1'=4,'col_0'=16,'col_1'=2] {'row_0','row_1'}, dimensions={0} | all-to-all | bytes 2097152 | tf_op jit(solution)/shard_map/all_to_all | solution.py:15
  31.4 1.4 broadcast_in_dim.5
  32.8 3.7 %all-to-all-start.1 = ((bf16[16,5,64,128]{3,2,1,0:T(8,128)(2,1)}), bf16[16,5,64,128]{3,2,1,0:T(8,128)(2,1)S(1)}, u32[]{:S(2)}, u32[]{:S(2)}) async-start(bf16[16,5,64,128]{3,2,1,0:T(8,128)(2,1)} %broadcast_in_dim.5), calls=%async_computation.1 | async-start | bytes 2621440 | tf_op jit(solution)/shard_map/all_to_all | solution.py:15
  39.0 14.3 %all-to-all-done.1 = bf16[16,5,64,128]{3,2,1,0:T(8,128)(2,1)S(1)} async-done(((bf16[16,5,64,128]{3,2,1,0:T(8,128)(2,1)}), bf16[16,5,64,128]{3,2,1,0:T(8,128)(2,1)S(1)}, u32[]{:S(2)}, u32[]{:S(2)}) %all-to-all-start.1) | async-done | bytes 1310752 | tf_op jit(solution)/shard_map/all_to_all | solution.py:15
  54.8 33.2 %all-gather.2.cloned.1.call-done = bf16[5,128,2048]{1,2,0:T(8,128)(2,1)} async-done(((bf16[5,128,64]{1,2,0:T(8,128)(2,1)}), bf16[5,128,2048]{1,2,0:T(8,128)(2,1)}) %all-gather.2.cloned.1.call-update) | async-done | bytes 2621456 | tf_op jit(solution)/shard_map/all_gather | solution.py:101
  88.0 3.0 %fusion.3 = f32[5,4,64,128]{3,2,0,1:T(8,128)S(1)} fusion(bf16[5,128,2048]{1,2,0:T(8,128)(2,1)} %all-gather.2.cloned.1.call-done, bf16[4,2048,64,1]{1,2,0,3:T(8,128)(2,1)} %reshape.95), kind=kOutput, calls=%fused_computation.5 | convolution fusion | flops 671088640 | bytes 4325376 | tf_op jit(solution)/shard_map/wax,txb->wtba/dot_general | solution.py:66
  91.1 4.0 %fusion.2 = bf16[5,4,64,128]{3,0,2,1:T(8,128)(2,1)S(1)} fusion(f32[5,4,64,128]{3,2,0,1:T(8,128)S(1)} %fusion.3, f32[5,4,5,4,1]{2,3,1,0,4:T(4,128)S(1)} %bitcast.73), kind=kOutput, calls=%fused_computation.4 | convolution fusion | flops 39485440 | bytes 984640 | tf_op jit(solution)/shard_map/vswt,wtba->vsba/dot_general | solution.py:70
  96.4 2.5 copy.24
  98.9 3.2 %copy.25 = bf16[2,16,4,128,64]{3,4,2,1,0:T(8,128)(2,1)} copy(bf16[2,16,4,128,64]{3,4,0,1,2:T(8,128)(2,1)} %bitcast.70) | data formatting | bytes 4194304 | tf_op jit(solution)/shard_map/transpose | solution.py:32
  102.1 17.6 %reduce-scatter.3.cloned.1.call-done = bf16[16,4,128,64]{2,3,1,0:T(8,128)(2,1)} async-done(((bf16[32,4,128,64]{2,3,1,0:T(8,128)(2,1)}), bf16[16,4,128,64]{2,3,1,0:T(8,128)(2,1)}) %reduce-scatter.3.cloned.1.call-update) | async-done | bytes 1048592 | tf_op jit(solution)/shard_map/reduce_scatter | solution.py:35
  122.4 61.7 %reduce-scatter.5.cloned.1.call-done = bf16[1,4,128,64]{2,3,1,0:T(8,128)(2,1)} async-done(((bf16[16,4,128,64]{2,3,1,0:T(8,128)(2,1)}), bf16[1,4,128,64]{2,3,1,0:T(8,128)(2,1)}) %reduce-scatter.5.cloned.1.call-update) | async-done | bytes 65552 | tf_op jit(solution)/shard_map/reduce_scatter | solution.py:35
  184.0 1.5 fusion.10
  190.8 8.6 %all-reduce.14 = (f32[4]{0:T(128)S(1)}, f32[4]{0:T(128)S(1)}, f32[4]{0:T(128)S(1)}) all-reduce(f32[4]{0:T(128)S(1)} %dynamic-update-slice.8, f32[4]{0:T(128)S(1)} %dynamic-update-slice, f32[4]{0:T(128)S(1)} %dynamic-update-slice.4), channel_id=1, replica_groups=mesh['row_0'=4,'row_1'=4,'col_0'=16,'col_1'=2] {'row_0'}, use_global_device_ids=true, to_apply=%add.8 | all-reduce | flops 12 | bytes 96
  200.6 1.4 dynamic-update-slice.5
  202.0 1.4 dynamic-update-slice.1
  204.0 1.4 dynamic-update-slice.9
  206.6 8.2 %all-reduce.13 = (f32[4]{0:T(128)S(1)}, f32[4]{0:T(128)S(1)}, f32[4]{0:T(128)S(1)}) all-reduce(f32[4]{0:T(128)S(1)} %dynamic-update-slice.9, f32[4]{0:T(128)S(1)} %dynamic-update-slice.1, f32[4]{0:T(128)S(1)} %dynamic-update-slice.5), channel_id=1, replica_groups=mesh['row_0'=4,'row_1'=4,'col_0'=16,'col_1'=2] {'row_1'}, use_global_device_ids=true, to_apply=%add.9 | all-reduce | flops 12 | bytes 96
  216.0 1.4 dynamic-update-slice.6
  217.4 1.4 dynamic-update-slice.2
  219.4 1.4 dynamic-update-slice.10
  220.8 21.5 %all-reduce.12 = (f32[16]{0:T(128)S(1)}, f32[16]{0:T(128)S(1)}, f32[16]{0:T(128)S(1)}) all-reduce(f32[16]{0:T(128)S(1)} %dynamic-update-slice.10, f32[16]{0:T(128)S(1)} %dynamic-update-slice.2, f32[16]{0:T(128)S(1)} %dynamic-update-slice.6), channel_id=1, replica_groups=mesh['row_0'=4,'row_1'=4,'col_0'=16,'col_1'=2] {'col_0'}, use_global_device_ids=true, to_apply=%add.10 | all-reduce | flops 48 | bytes 384
  244.8 1.4 dynamic-update-slice.3
  248.1 23.9 %all-reduce.15 = (f32[2]{0:T(128)S(1)}, f32[2]{0:T(128)S(1)}, f32[2]{0:T(128)S(1)}) all-reduce(f32[2]{0:T(128)S(1)} %dynamic-update-slice.11, f32[2]{0:T(128)S(1)} %dynamic-update-slice.3, f32[2]{0:T(128)S(1)} %dynamic-update-slice.7), channel_id=1, replica_groups=mesh['row_0'=4,'row_1'=4,'col_0'=16,'col_1'=2] {'col_1'}, use_global_device_ids=true, to_apply=%add.11 | all-reduce | flops 6 | bytes 48
  277.7 1.5 fusion.13
  (56 shorter events, 24.9 us)
Async XLA Ops:
  7.2 29.4 %copy-start = (f32[5,5,2,2]{1,3,2,0:T(2,128)S(1)}, f32[5,5,2,2]{1,3,2,0:T(2,128)}, u32[]{:S(2)}) copy-start(f32[5,5,2,2]{1,3,2,0:T(2,128)} %param.8) | copy-start | bytes 1204
  7.2 24.2 %copy-start.2 = (bf16[5,64,128]{2,1,0:T(8,128)(2,1)S(1)}, bf16[5,64,128]{2,1,0:T(8,128)(2,1)}, u32[]{:S(2)}) copy-start(bf16[5,64,128]{2,1,0:T(8,128)(2,1)} %param.7) | copy-start | bytes 245764
  7.2 80.8 %all-gather.2.cloned.1.call-start = ((), (), s32[]{:S(2)}) async-start(), calls=%async_computation.4 | async-start | bytes 2703360 | tf_op jit(solution)/shard_map/all_gather | solution.py:101
  31.4 5.2 %copy-start.3 = (f32[5,5,2,2]{1,3,2,0:T(2,128)S(1)}, f32[5,5,2,2]{1,3,2,0:T(2,128)}, u32[]{:S(2)}) copy-start(f32[5,5,2,2]{1,3,2,0:T(2,128)} %param.9) | copy-start | bytes 1204
  32.8 20.5 %all-to-all-start.1 = ((bf16[16,5,64,128]{3,2,1,0:T(8,128)(2,1)}), bf16[16,5,64,128]{3,2,1,0:T(8,128)(2,1)S(1)}, u32[]{:S(2)}, u32[]{:S(2)}) async-start(bf16[16,5,64,128]{3,2,1,0:T(8,128)(2,1)} %broadcast_in_dim.5), calls=%async_computation.1 | async-start | bytes 2621440 | tf_op jit(solution)/shard_map/all_to_all | solution.py:15
  36.5 83.2 %reduce-scatter.3.cloned.1.call-start = ((), (), s32[]{:S(2)}) async-start(), calls=%async_computation.5 | async-start | bytes 3145728 | tf_op jit(solution)/shard_map/reduce_scatter | solution.py:35
  102.1 82.0 %copy-start.1 = (bf16[4,128,64]{1,2,0:T(8,128)(2,1)S(1)}, bf16[4,128,64]{1,2,0:T(8,128)(2,1)}, u32[]{:S(2)}) copy-start(bf16[4,128,64]{1,2,0:T(8,128)(2,1)} %param.5) | copy-start | bytes 196612
  102.1 82.0 %reduce-scatter.5.cloned.1.call-start = ((), (), s32[]{:S(2)}) async-start(), calls=%async_computation.6 | async-start | bytes 1114112 | tf_op jit(solution)/shard_map/reduce_scatter | solution.py:35
Sparse Core Ops, SparseCore 0:
  10.1 77.8 all-gather.1
  102.2 17.5 reduce-scatter.2
  122.6 61.4 reduce-scatter.4
